TPU v7x, 32 devices: a whole 2x2x4 slice. The times are simulated.
32 devices in a mesh: group: 2 (over y), pages: 4 (over z), heads: 4 (over x, core).
Axes of the slice: x: 2, y: 2, z: 4, core: 2. Of those that a mesh axis runs over, the one named last changes fastest.
Arguments:
- queries: bfloat16 [16, 48, 128], P('group', 'heads'), parts along dimension 0, may hold values from -180 to 180
- k_cache: bfloat16 [8, 16384, 16, 128], P('heads', ('group', 'pages')), parts along dimension 1, may hold values from -6 to 6
- v_cache: bfloat16 [8, 16384, 16, 128], P('heads', ('group', 'pages')), parts along dimension 1, may hold values from -6 to 6
- new_key: bfloat16 [8, 16, 128], P('heads', 'group'), parts along dimension 1, may hold values from -6 to 6
- new_value: bfloat16 [8, 16, 128], P('heads', 'group'), parts along dimension 1, may hold values from -6 to 6
- ctx_lens: int32 [16], P('group'), parts along dimension 0, may hold values from 4081 to 16384, as said below
- page_owner: int32 [16, 1024], P('group'), parts along dimension 0, may hold values from -1 to 3, as said below
- page_slot: int32 [16, 1024], P('group'), parts along dimension 0, may hold values from 0 to 2047, as said below
- out_weight: bfloat16 [6144, 6144], P(None, 'pages'), may hold values from -0.078125 to 0.078125
Outputs:
- projected: bfloat16 [16, 6144], P(('group', 'heads'), 'pages'), parts along dimension 0
There are 2 independent parts, one for each index of `group`. A program takes and returns all parts, laid end to end along the dimension named above; an argument that names none is the same for every part. Nothing has to cross between parts.
Inputs may be any that keep to these rules, and one draw needn't show every extreme that they name: Request r holds ceil(ctx_lens[r] / 16) pages; some request holds 16384 tokens. `page_owner`: for j below request r's page count, the device along pages that holds its logical page j; -1 beyond. No two live pages share a device and a slot. `page_slot`: for j below request r's page count, the slot of logical page j on its device; 0 beyond.
All inputs are finite; a program needn't handle non-finite values.
Results may differ from a plain program's by a relative error of at most 0.0053.
Values may be sent and summed in bfloat16 or wider, within the bound.
A program may use at most 128 MiB of HBM per device.

v0:
```python
import math

import jax
import jax.numpy as jnp
from jax import lax
from jax.sharding import PartitionSpec as P

very_low = -1e30
highest = lax.Precision.HIGHEST


def combine_pages(peak_score, partial_out, weight_sum):
    whole_peak = lax.pmax(peak_score, "pages")
    factor = jnp.exp(peak_score - whole_peak)
    summed_out, summed_weight = lax.psum(
        (partial_out * factor[..., None], weight_sum * factor), "pages"
    )
    return (whole_peak, summed_out, summed_weight)


def finish(peak_score, partial_out, weight_sum, self_score, self_value, group_size):
    expanded = jnp.repeat(self_value, group_size, axis=1)
    peak_value = jnp.maximum(peak_score, self_score)
    keep_old = jnp.exp(peak_score - peak_value)
    take_new = jnp.exp(self_score - peak_value)
    attended = (partial_out * keep_old[..., None] + expanded * take_new[..., None]) / (
        weight_sum * keep_old + take_new
    )[..., None]
    return attended.astype(jnp.bfloat16)


def slot_tables(target, entry_request, entry_page, entry_length, slot_count):
    block_size = math.gcd(slot_count, 128)
    block_count = slot_count // block_size

    def one_block(block_number):
        slot_numbers = block_number * block_size + jnp.arange(block_size, dtype=jnp.int32)
        matched = target[None, :] == slot_numbers[:, None]
        owner = jnp.max(jnp.where(matched, entry_request[None, :], -1), axis=1)
        page_number = jnp.max(jnp.where(matched, entry_page[None, :], 0), axis=1)
        length = jnp.max(jnp.where(matched, entry_length[None, :], 0), axis=1)
        return (owner, page_number, length)

    owners, pages_found, lengths_found = lax.map(
        one_block, jnp.arange(block_count, dtype=jnp.int32)
    )
    return (
        owners.reshape(slot_count),
        pages_found.reshape(slot_count),
        lengths_found.reshape(slot_count),
    )


def local(
    queries, k_cache, v_cache, new_key, new_value, ctx_lens, page_owner, page_slot, out_weight
):
    kv_local, slot_count, page_rows, head_dim = k_cache.shape
    requests, q_local, _ = queries.shape
    group_size = q_local // kv_local
    max_pages = page_owner.shape[1]
    scaling = 1.0 / math.sqrt(head_dim)
    page_index = lax.axis_index("pages")
    request_ids = jnp.broadcast_to(jnp.arange(requests, dtype=jnp.int32)[:, None], page_owner.shape)
    page_ids = jnp.broadcast_to(jnp.arange(max_pages, dtype=jnp.int32)[None, :], page_owner.shape)
    entry_length = jnp.broadcast_to(ctx_lens[:, None], page_owner.shape)
    target = jnp.where(page_owner == page_index, page_slot, slot_count).reshape(-1)
    slot_request, slot_page, slot_length = slot_tables(
        target, request_ids.reshape(-1), page_ids.reshape(-1), entry_length.reshape(-1), slot_count
    )
    position = slot_page[:, None] * page_rows + jnp.arange(page_rows, dtype=jnp.int32)[None, :]
    live_mask = (position < slot_length[:, None])[:, None, None, :]
    belongs = slot_request[None, :] == jnp.arange(requests, dtype=jnp.int32)[:, None]
    belongs_low = belongs.astype(jnp.bfloat16)
    slot_query = (
        jnp.dot(
            belongs_low.T,
            queries.reshape(requests, q_local * head_dim),
            preferred_element_type=jnp.float32,
        )
        .astype(jnp.bfloat16)
        .reshape(slot_count, kv_local, group_size, head_dim)
    )
    grouped = queries.reshape(requests, kv_local, group_size, head_dim)
    scores = (
        jnp.einsum("pkgd,kptd->pkgt", slot_query, k_cache, preferred_element_type=jnp.float32)
        * scaling
    )
    scores = jnp.where(live_mask, scores, very_low)
    page_top = jnp.max(scores, axis=3)
    weights = jnp.where(live_mask, jnp.exp(scores - page_top[..., None]), 0.0)
    page_total = jnp.sum(weights, axis=3)
    page_out = jnp.einsum(
        "pkgt,kptd->pkgd", weights.astype(jnp.bfloat16), v_cache, preferred_element_type=jnp.float32
    )
    flat_top = page_top.reshape(slot_count, q_local)
    device_top = jnp.max(jnp.where(belongs[:, :, None], flat_top[None, :, :], very_low), axis=1)
    slot_top = jnp.max(jnp.where(belongs[:, :, None], device_top[:, None, :], very_low), axis=0)
    factor = jnp.exp(flat_top - slot_top)
    scaled = page_out.reshape(slot_count, q_local * head_dim) * jnp.repeat(factor, head_dim, axis=1)
    belongs_float = belongs.astype(jnp.float32)
    device_out = jnp.dot(
        belongs_float, scaled, precision=highest, preferred_element_type=jnp.float32
    ).reshape(requests, q_local, head_dim)
    device_sum = jnp.dot(
        belongs_float,
        page_total.reshape(slot_count, q_local) * factor,
        precision=highest,
        preferred_element_type=jnp.float32,
    )
    self_score = (
        jnp.einsum("rkgd,krd->rkg", grouped, new_key, preferred_element_type=jnp.float32).reshape(
            requests, q_local
        )
        * scaling
    )
    self_value = jnp.transpose(new_value, (1, 0, 2)).astype(jnp.float32)
    peak_score, partial_out, weight_sum = combine_pages(device_top, device_out, device_sum)
    attended = finish(peak_score, partial_out, weight_sum, self_score, self_value, group_size)
    head_rows = lax.all_to_all(attended, "heads", split_axis=0, concat_axis=1, tiled=True)
    flat_rows = head_rows.reshape(head_rows.shape[0], head_rows.shape[1] * head_rows.shape[2])
    return jnp.dot(flat_rows, out_weight, preferred_element_type=jnp.float32).astype(jnp.bfloat16)


def solution(mesh):
    placed = (
        P("group", "heads", None),
        P("heads", ("group", "pages"), None, None),
        P("heads", ("group", "pages"), None, None),
        P("heads", "group", None),
        P("heads", "group", None),
        P("group"),
        P("group", None),
        P("group", None),
        P(None, "pages"),
    )
    return jax.shard_map(
        local, mesh=mesh, in_specs=placed, out_specs=P(("group", "heads"), "pages"), check_vma=False
    )
```

profile of v0, /device:TPU:0, one launch (start us, length us, event | category | flops | bytes accessed | tf_op | source)
XLA Modules:
  0.0 275.0 jit_solution(18116491772527730561)
XLA Ops:
  0.8 69.5 %while.15 = (s32[]{:T(128)}, s32[16,128]{1,0:T(8,128)S(1)}, s32[16,128]{1,0:T(8,128)S(1)}, s32[16,128]{1,0:T(8,128)S(1)}, s32[8,1024]{1,0:T(8,128)S(1)}, /*index...) while((s32[]{:T(128)}, s32[16,128]{1,0:T(8,128)S(1)}, ...), condition=%wide.region_4.5_spmd.clone, body=%wide.region_0.4_spmd.clone.sunk | while | flops 7339779 | bytes 497325 | solution.py:44
  3.0 2.1 fusion.46
  7.3 2.1 fusion.46
  11.6 2.1 fusion.46
  16.0 2.1 fusion.46
  20.3 2.1 fusion.46
  24.7 2.1 fusion.46
  29.0 2.1 fusion.46
  33.3 2.1 fusion.46
  37.7 2.1 fusion.46
  42.0 2.1 fusion.46
  46.4 2.1 fusion.46
  50.7 2.1 fusion.46
  55.1 2.1 fusion.46
  59.4 2.1 fusion.46
  63.7 2.1 fusion.46
  68.1 2.1 fusion.46
  70.3 5.2 %convolution_convert_fusion = bf16[2048,1536]{0,1:T(8,128)(2,1)} fusion(s32[2048]{0:T(1024)S(1)} %bitcast.88, bf16[8,12,128]{2,0,1:T(8,128)(2,1)} %param.11), kind=kOutput, calls=%fused_computation.32 | convolution fusion | flops 53493760 | bytes 6324224 | tf_op jit(solution)/shard_map/dot_general | solution.py:75
  75.5 11.9 %copy.42 = bf16[2048,2,6,128]{3,2,1,0:T(8,128)(2,1)} copy(bf16[2048,2,6,128]{0,3,2,1:T(8,128)(2,1)} %bitcast.85) | data formatting | bytes 12582912 | tf_op jit(solution)/shard_map/reshape | solution.py:81
  87.4 1.3 add_compare_fusion
  88.7 21.7 %fusion.13 = (f32[2048,2,6]{2,1,0:T(2,128)S(1)}, f32[2048,2,6,16]{3,2,1,0:T(8,128)}) fusion(pred[2048,16]{1,0:T(8,128)(4,1)S(1)} %add_compare_fusion, bf16[2048,2,6,128]{3,2,1,0:T(8,128)(2,1)} %copy.42, bf16[2,2048,16,128]{3,2,1,0:T(8,128)(2,1)} %param.12), kind=kOutput, calls=%fused_computation.23 | convolution fusion | flops 101818368 | bytes 24772608 | tf_op jit(solution)/shard_map/pkgd,kptd->pkgt/dot_general | solution.py:85
  110.5 0.9 copy.46
  112.0 13.5 %pmax.7 = f32[8,12]{1,0:T(8,128)S(1)} all-reduce(f32[8,12]{1,0:T(8,128)S(1)} %copy.48), channel_id=1, replica_groups=mesh['group'=2,'pages'=4,'heads'=4] {'pages'}, use_global_device_ids=true, to_apply=%region_8.9 | all-reduce | flops 96 | bytes 768 | tf_op jit(solution)/shard_map/pmax | solution.py:13
  125.5 60.2 %fusion.14 = f32[2048,2,6]{2,1,0:T(2,128)} fusion(f32[2048,2,6,16]{3,2,1,0:T(8,128)} %get-tuple-element.103, f32[2048,2,6]{2,1,0:T(2,128)S(1)} %get-tuple-element.102, pred[2048,16]{1,0:T(8,128)(4,1)S(1)} %add_compare_fusion), kind=kLoop, calls=%fused_computation.25 | loop fusion | flops 1941504 | bytes 1802240 | tf_op jit(solution)/shard_map/reduce_sum | solution.py:91
  185.7 2.7 copy.52
  188.5 17.7 %fusion.9 = f32[2048,2,6,128]{3,2,1,0:T(8,128)} fusion(bf16[2,2048,16,128]{3,2,1,0:T(8,128)(2,1)} %param.13, f32[2048,2,6,16]{3,2,1,0:T(8,128)} %get-tuple-element.103, f32[2048,2,6]{2,1,0:T(2,128)S(1)} %get-tuple-element.102, pred[2048,16]{1,0:T(8,128)(4,1)S(1)} %add_compare_fusion), kind=kOutput, calls=%fused_computation.17 | convolution fusion | flops 102629376 | bytes 31064064 | tf_op jit(solution)/shard_map/pkgt,kptd->pkgd/dot_general | solution.py:92
  206.1 16.1 %copy.45 = f32[2048,2,6,128]{0,3,2,1:T(8,128)} copy(f32[2048,2,6,128]{3,2,1,0:T(8,128)} %fusion.9) | data formatting | bytes 25165824 | tf_op jit(solution)/shard_map/pkgt,kptd->pkgd/dot_general | solution.py:92
  222.4 12.1 %bitcast_multiply_fusion = f32[2048,1536]{0,1:T(8,128)} fusion(f32[2048,2,6,128]{0,3,2,1:T(8,128)} %copy.45, f32[2048,12]{0,1:T(8,128)S(1)} %subtract_exponential_fusion), kind=kLoop, calls=%fused_computation.24 | loop fusion | flops 3145728 | bytes 25264128 | tf_op jit(solution)/shard_map/mul | solution.py:99
  234.7 8.7 %convolution_multiply_fusion = f32[8,12,128]{2,0,1:T(8,128)S(1)} fusion(f32[12,128,2048]{2,1,0:T(8,128)} %bitcast.84, s32[2048]{0:T(1024)S(1)} %bitcast.90, f32[8,12]{0,1:T(8,128)S(1)} %copy.49), kind=kOutput, calls=%fused_computation.34 | convolution fusion | flops 302018560 | bytes 12640640 | tf_op jit(solution)/shard_map/dot_general | solution.py:101
  243.4 16.4 %all-reduce = (f32[8,12,128]{2,0,1:T(8,128)S(1)}, f32[8,12]{1,0:T(8,128)S(1)}) all-reduce(f32[8,12,128]{2,0,1:T(8,128)S(1)} %convolution_multiply_fusion, f32[8,12]{1,0:T(8,128)S(1)} %convolution_multiply_fusion.1), channel_id=1, replica_groups=mesh['group'=2,'pages'=4,'heads'=4] {'pages'}, use_global_device_ids=true, to_apply=%region_9.10 | all-reduce | flops 12384 | bytes 99072 | tf_op jit(solution)/shard_map/psum | solution.py:15
  260.2 6.5 %all_to_all.15 = bf16[8,12,128]{2,1,0:T(8,128)(2,1)S(1)} all-to-all(bf16[8,12,128]{2,1,0:T(8,128)(2,1)S(1)} %copy.54), channel_id=1, replica_groups=mesh['group'=2,'pages'=4,'heads'=4] {'heads'}, dimensions={0} | all-to-all | bytes 49152 | tf_op jit(solution)/shard_map/all_to_all | solution.py:119
  266.7 8.3 %convolution_convert_fusion.1 = bf16[2,1536]{1,0:T(2,128)(2,1)} fusion(bf16[2,6144]{1,0:T(2,128)(2,1)S(1)} %reshape.121, bf16[6144,1536]{1,0:T(8,128)(2,1)} %param.19), kind=kOutput, calls=%fused_computation.33 | convolution fusion | flops 37751808 | bytes 18905088 | tf_op jit(solution)/shard_map/dot_general | solution.py:121
  (194 shorter events, 27.1 us)
Async XLA Ops:
  0.0 234.5 %copy-start = (bf16[2,8,128]{2,1,0:T(8,128)(2,1)S(1)}, bf16[2,8,128]{2,1,0:T(8,128)(2,1)}, u32[]{:S(2)}) copy-start(bf16[2,8,128]{2,1,0:T(8,128)(2,1)} %param.14) | copy-start | bytes 12292
  222.2 12.3 %copy-start.1 = (bf16[8,12,128]{2,0,1:T(8,128)(2,1)S(1)}, bf16[8,12,128]{2,0,1:T(8,128)(2,1)}, u32[]{:S(2)}) copy-start(bf16[8,12,128]{2,0,1:T(8,128)(2,1)} %param.11) | copy-start | bytes 73732
  222.4 37.6 %copy-start.2 = (bf16[2,8,128]{2,1,0:T(8,128)(2,1)S(1)}, bf16[2,8,128]{2,1,0:T(8,128)(2,1)}, u32[]{:S(2)}) copy-start(bf16[2,8,128]{2,1,0:T(8,128)(2,1)} %param.15) | copy-start | bytes 12292
where the time goes:
time: 276 us; the launch traced here: 275 us
  other arithmetic  108 us (39%)
  matrix products  61.9 us (22%)
  local copies, waits for them, and re-layouts  56.9 us (21%)
  blocking collectives  36.4 us (13%)
  loops' own time  11.8 us (4%)
    reduce_sum x1, other arithmetic, local(): page_total = jnp.sum(weights, axis=3)  60.2 us
    reduce_max x16, other arithmetic, one_block(): length = jnp.max(jnp.where(matched, entry_length[None, :], 0), axis=1)  32.9 us
    dot_general x1, matrix products, local(): jnp.einsum('pkgd,kptd->pkgt', slot_query, k_cache, preferred_element_type...  21.7 us
    dot_general x1, matrix products, local(): jnp.einsum('pkgt,kptd->pkgd', weights.astype(jnp.bfloat16), v_cache, pref...  17.7 us
    psum x1, blocking collectives, combine_pages(): lax.psum((partial_out * factor[..., None], weight_sum * factor), 'pages')  16.4 us
    dot_general x1, local copies, waits for them, and re-layouts, local(): jnp.einsum('pkgt,kptd->pkgd', weights.astype(jnp.bfloat16), v_cache, pref...  16.1 us
    pmax x1, blocking collectives, combine_pages(): whole_peak = lax.pmax(peak_score, 'pages')  13.5 us
    mul x1, other arithmetic, local(): page_out.reshape(slot_count, q_local * head_dim)  12.1 us

commit v1 on v0

v1 whole, which is shorter than its diff:
```python
import functools
import math

import jax
import jax.numpy as jnp
from jax import lax
from jax.experimental import pallas as pl
from jax.experimental.pallas import tpu as pltpu
from jax.sharding import PartitionSpec as P

MESH = pl.DeviceIdType.MESH
very_low = -1e30
NT = (((1,), (1,)), ((), ()))


def round_up(value, unit):
    return (value + unit - 1) // unit * unit


def attend_kernel(
    cfg, q_ref, owner_ref, slot_ref, len_ref, k_ref, v_ref, part_ref, buf, s_ref, tok, mx, acc, lsum, ksem, vsem
):
    kv, rows, reqs, blocks, group, page_rows, pages, per_chunk, chunks, factor = cfg
    tokens = per_chunk * page_rows
    depth = q_ref.shape[2]
    own_reqs = reqs // blocks
    kv_block = group * own_reqs
    half = part_ref.shape[1] // 2

    def copy_in(source, sem, c):
        start = pl.multiple_of(c * tokens, tokens)
        return pltpu.make_async_copy(source.at[:, pl.ds(start, tokens)], buf.at[c], sem.at[c])

    for c in range(chunks):
        copy_in(k_ref, ksem, c).start()

    me = lax.axis_index("pages")
    page_id = lax.broadcasted_iota(jnp.int32, (reqs, pages), 1)
    slot = slot_ref[...]
    upper = jnp.where(owner_ref[...] == me, slot // per_chunk, -1)
    lower = slot % per_chunk
    live = jnp.clip(len_ref[...] - page_id * page_rows, 0, page_rows).astype(jnp.float32)
    upper_id = lax.broadcasted_iota(jnp.int32, (chunks, pages), 0)
    lower_id = lax.broadcasted_iota(jnp.int32, (per_chunk, pages), 0)
    table = jnp.zeros((2 * chunks, per_chunk), jnp.float32)
    for r in range(reqs):
        hit = upper[r : r + 1] == upper_id
        left = jnp.concatenate(
            [jnp.where(hit, float(r + 1), 0.0), jnp.where(hit, live[r : r + 1], 0.0)], axis=0
        ).astype(jnp.bfloat16)
        right = jnp.where(lower[r : r + 1] == lower_id, 1.0, 0.0).astype(jnp.bfloat16)
        table += lax.dot_general(left, right, NT, preferred_element_type=jnp.float32)
    spread = jnp.where(
        lax.broadcasted_iota(jnp.int32, (per_chunk, tokens), 1) // page_rows
        == lax.broadcasted_iota(jnp.int32, (per_chunk, tokens), 0),
        1.0,
        0.0,
    ).astype(jnp.bfloat16)
    wide = jnp.dot(table.astype(jnp.bfloat16), spread, preferred_element_type=jnp.float32)
    row_number = (lax.broadcasted_iota(jnp.int32, (chunks, tokens), 1) % page_rows).astype(jnp.float32)
    token_owner = jnp.where(row_number < wide[chunks:], wide[:chunks], 0.0)
    for c in range(chunks):
        tok[c] = jnp.broadcast_to(token_owner[c : c + 1], (8, tokens))

    row_id = lax.broadcasted_iota(jnp.int32, (rows, 128), 0)
    row_req = (row_id // kv_block * own_reqs + row_id % own_reqs + 1).astype(jnp.float32)
    mx[...] = jnp.full_like(mx, very_low)
    acc[...] = jnp.zeros_like(acc)
    lsum[...] = jnp.zeros_like(lsum)
    sub = min(tokens, 512)

    def score_chunk(c, carry):
        copy_in(k_ref, ksem, c).wait()
        for n in range(kv):
            best = [mx[n, 8 * g : 8 * g + 8] for g in range(rows // 8)]
            for b in range(tokens // sub):
                s = lax.dot_general(
                    q_ref[n], buf[c, n, b * sub : (b + 1) * sub, :], NT, preferred_element_type=jnp.float32
                )
                for t in range(sub // 128):
                    at = b * sub + t * 128
                    who = tok[c, :, at : at + 128]
                    for g in range(rows // 8):
                        kept = jnp.where(
                            who == row_req[8 * g : 8 * g + 8],
                            s[8 * g : 8 * g + 8, t * 128 : t * 128 + 128],
                            very_low,
                        )
                        s_ref[c, n, 8 * g : 8 * g + 8, at : at + 128] = kept
                        best[g] = jnp.maximum(best[g], kept)
            for g in range(rows // 8):
                mx[n, 8 * g : 8 * g + 8] = best[g]
        copy_in(v_ref, vsem, c).start()
        return carry

    lax.fori_loop(0, chunks, score_chunk, 0)
    top = jnp.max(mx[...], axis=2, keepdims=True)
    mx[...] = jnp.broadcast_to(top, mx.shape)

    def value_chunk(c, carry):
        copy_in(v_ref, vsem, c).wait()
        for n in range(kv):
            peak = mx[n]
            total = lsum[n]
            out = acc[n]
            for b in range(tokens // sub):
                parts = []
                for t in range(sub // 128):
                    at = b * sub + t * 128
                    w = jnp.exp2((s_ref[c, n, :, at : at + 128] - peak) * factor)
                    total += w
                    parts.append(w.astype(jnp.bfloat16))
                out += jnp.dot(
                    jnp.concatenate(parts, axis=1),
                    buf[c, n, b * sub : (b + 1) * sub, :],
                    preferred_element_type=jnp.float32,
                )
            lsum[n] = total
            acc[n] = out
        return carry

    lax.fori_loop(0, chunks, value_chunk, 0)
    lane = lax.broadcasted_iota(jnp.int32, (rows, 128), 1)
    part_ref[...] = jnp.zeros_like(part_ref)
    for n in range(kv):
        stats = jnp.where(lane == 0, mx[n], jnp.sum(lsum[n], axis=1, keepdims=True))
        out = acc[n]
        for p in range(blocks):
            here = slice(p * kv_block, (p + 1) * kv_block)
            part_ref[p, n * kv_block : (n + 1) * kv_block, :] = out[here]
            part_ref[p, half + n * kv_block : half + (n + 1) * kv_block, :] = stats[here]


def project_kernel(
    cfg, part_ref, q_ref, key_ref, value_ref, w_ref, y_ref,
    wbuf, got, mine, rows_in, lhs, total, wsem, send_a, recv_a, send_b, recv_b,
):
    pages, heads, reqs, head_count, pieces, factor = cfg
    group = lax.axis_index("group")
    p = lax.axis_index("pages")
    h = lax.axis_index("heads")
    half = part_ref.shape[1] // 2
    own_reqs = reqs // pages
    out_reqs = reqs // heads
    shares = pages // heads
    depth = part_ref.shape[2]
    piece_rows = wbuf.shape[1]

    def weight_copy(i):
        return pltpu.make_async_copy(
            w_ref.at[pl.ds(pl.multiple_of(i * piece_rows, piece_rows), piece_rows)], wbuf.at[i], wsem.at[i]
        )

    for i in range(pieces):
        weight_copy(i).start()

    barrier = pltpu.get_barrier_semaphore()
    count = pages * heads
    for k in range(1, count):
        other = lax.rem(p * heads + h + k, count)
        pl.semaphore_signal(
            barrier, inc=1, device_id=(group, other // heads, lax.rem(other, heads)), device_id_type=MESH
        )

    q = q_ref[p]
    self_score = jnp.sum(q * key_ref[p], axis=1, keepdims=True)
    pl.semaphore_wait(barrier, count - 1)

    def exchange(k):
        to = lax.rem(p + k, pages)
        return pltpu.make_async_remote_copy(
            src_ref=part_ref.at[to],
            dst_ref=got.at[k - 1],
            send_sem=send_a.at[k - 1],
            recv_sem=recv_a.at[k - 1],
            device_id=(group, to, h),
            device_id_type=MESH,
        )

    for k in range(1, pages):
        exchange(k).start()
    for k in range(1, pages):
        exchange(k).wait_recv()

    tops = [part_ref[p, half:, 0:1]] + [got[k, half:, 0:1] for k in range(pages - 1)]
    sums = [part_ref[p, half:, 1:2]] + [got[k, half:, 1:2] for k in range(pages - 1)]
    outs = [part_ref[p, :half]] + [got[k, :half] for k in range(pages - 1)]
    peak = self_score
    for t in tops:
        peak = jnp.maximum(peak, t)
    take = jnp.exp2((self_score - peak) * factor)
    out = take * value_ref[p]
    weight = take
    for t, s, o in zip(tops, sums, outs):
        f = jnp.exp2((t - peak) * factor)
        out += f * o
        weight += f * s
    attended = (out / weight).astype(jnp.bfloat16)
    mine[...] = jnp.zeros_like(mine)
    mine[0:half, :] = attended

    target = p // shares
    place = lax.rem(p, shares) * heads + h

    def hand_over(k):
        to = lax.rem(p + k, pages)
        return pltpu.make_async_remote_copy(
            src_ref=mine,
            dst_ref=rows_in.at[place],
            send_sem=send_b.at[k],
            recv_sem=recv_b.at[place],
            device_id=(group, to, target),
            device_id_type=MESH,
        )

    for k in range(pages):
        if k == 0:
            pl.when(target != h)(lambda: hand_over(0).start())

            @pl.when(target == h)
            def _():
                rows_in[place] = mine[...]
        else:
            hand_over(k).start()

    def arrival(source):
        return pltpu.make_async_remote_copy(
            src_ref=mine,
            dst_ref=rows_in.at[source],
            send_sem=send_b.at[0],
            recv_sem=recv_b.at[source],
            device_id=(group, p, target),
            device_id_type=MESH,
        )

    for source in range(shares * heads):
        remote = jnp.logical_or(target != h, place != source)
        pl.when(remote)(lambda source=source: arrival(source).wait_recv())

    lhs[...] = jnp.zeros_like(lhs)
    per_piece = piece_rows // depth
    for source in range(shares * heads):
        first = source // heads * own_reqs
        block = rows_in[source].astype(jnp.float32)
        for n in range(head_count):
            which = source % heads * head_count + n
            col = which % per_piece * depth
            lhs[which // per_piece, first : first + own_reqs, col : col + depth] = block[
                n * own_reqs : (n + 1) * own_reqs
            ]
    total[...] = jnp.zeros_like(total)

    def multiply(i, carry):
        weight_copy(i).wait()
        total[...] += jnp.dot(
            lhs[i].astype(jnp.bfloat16), wbuf[i], preferred_element_type=jnp.float32
        )
        return carry

    lax.fori_loop(0, pieces, multiply, 0)
    y_ref[...] = total[0:out_reqs].astype(jnp.bfloat16)
    for k in range(1, pages):
        exchange(k).wait_send()
    pl.when(target != h)(lambda: hand_over(0).wait_send())
    for k in range(1, pages):
        hand_over(k).wait_send()


def local(sizes, queries, k_cache, v_cache, new_key, new_value, ctx_lens, page_owner, page_slot, out_weight):
    pages, heads = sizes
    kv, slots, page_rows, depth = k_cache.shape
    reqs, q_local, _ = queries.shape
    group = q_local // kv
    max_pages = page_owner.shape[1]
    factor = math.log2(math.e) / math.sqrt(depth)
    per_chunk = math.gcd(slots, 128)
    chunks = slots // per_chunk
    tokens = per_chunk * page_rows
    rows = group * reqs
    own_reqs = reqs // pages
    block = kv * group * own_reqs
    half = round_up(block, 8)
    vmem = pl.BlockSpec(memory_space=pltpu.VMEM)
    hbm = pl.BlockSpec(memory_space=pl.ANY)

    split = queries.reshape(pages, own_reqs, kv, group, depth)
    q_rows = split.transpose(2, 0, 3, 1, 4).reshape(kv, rows, depth)
    cfg = (kv, rows, reqs, pages, group, page_rows, max_pages, per_chunk, chunks, factor)
    part = pl.pallas_call(
        functools.partial(attend_kernel, cfg),
        out_shape=jax.ShapeDtypeStruct((pages, 2 * half, depth), jnp.float32),
        in_specs=[vmem] * 4 + [hbm] * 2,
        out_specs=vmem,
        scratch_shapes=[
            pltpu.VMEM((chunks, kv, tokens, depth), jnp.bfloat16),
            pltpu.VMEM((chunks, kv, rows, tokens), jnp.float32),
            pltpu.VMEM((chunks, 8, tokens), jnp.float32),
            pltpu.VMEM((kv, rows, 128), jnp.float32),
            pltpu.VMEM((kv, rows, depth), jnp.float32),
            pltpu.VMEM((kv, rows, 128), jnp.float32),
            pltpu.SemaphoreType.DMA((chunks,)),
            pltpu.SemaphoreType.DMA((chunks,)),
        ],
        compiler_params=pltpu.CompilerParams(vmem_limit_bytes=48 * 1024 * 1024),
        name="attend",
    )(
        q_rows,
        page_owner,
        page_slot,
        ctx_lens.reshape(reqs, 1),
        k_cache.reshape(kv, slots * page_rows, depth),
        v_cache.reshape(kv, slots * page_rows, depth),
    )

    def padded(x):
        return jnp.pad(x.astype(jnp.float32), ((0, 0), (0, half - block), (0, 0)))

    q_block = padded(split.transpose(0, 2, 3, 1, 4).reshape(pages, block, depth))

    def spread(x):
        y = x.reshape(kv, pages, 1, own_reqs, depth).transpose(1, 0, 2, 3, 4)
        return padded(jnp.broadcast_to(y, (pages, kv, group, own_reqs, depth)).reshape(pages, block, depth))

    model, columns = out_weight.shape
    pieces = math.gcd(model // depth, 8)
    shares = pages // heads
    out_reqs = reqs // heads
    lines = round_up(half, 16)
    cfg = (pages, heads, reqs, q_local, pieces, factor)
    return pl.pallas_call(
        functools.partial(project_kernel, cfg),
        out_shape=jax.ShapeDtypeStruct((out_reqs, columns), jnp.bfloat16),
        in_specs=[vmem] * 4 + [hbm],
        out_specs=vmem,
        scratch_shapes=[
            pltpu.VMEM((pieces, model // pieces, columns), jnp.bfloat16),
            pltpu.VMEM((pages - 1, 2 * half, depth), jnp.float32),
            pltpu.VMEM((lines, depth), jnp.bfloat16),
            pltpu.VMEM((shares * heads, lines, depth), jnp.bfloat16),
            pltpu.VMEM((pieces, 8, model // pieces), jnp.float32),
            pltpu.VMEM((8, columns), jnp.float32),
            pltpu.SemaphoreType.DMA((pieces,)),
            pltpu.SemaphoreType.DMA((pages - 1,)),
            pltpu.SemaphoreType.DMA((pages - 1,)),
            pltpu.SemaphoreType.DMA((pages,)),
            pltpu.SemaphoreType.DMA((shares * heads,)),
        ],
        compiler_params=pltpu.CompilerParams(
            collective_id=0, has_side_effects=True, vmem_limit_bytes=40 * 1024 * 1024
        ),
        name="project",
    )(part, q_block, spread(new_key), spread(new_value), out_weight)


def solution(mesh):
    placed = (
        P("group", "heads", None),
        P("heads", ("group", "pages"), None, None),
        P("heads", ("group", "pages"), None, None),
        P("heads", "group", None),
        P("heads", "group", None),
        P("group"),
        P("group", None),
        P("group", None),
        P(None, "pages"),
    )
    sizes = (mesh.shape["pages"], mesh.shape["heads"])
    return jax.shard_map(
        functools.partial(local, sizes),
        mesh=mesh,
        in_specs=placed,
        out_specs=P(("group", "heads"), "pages"),
        check_vma=False,
    )
```

time: 276 us -> 35.1 us (0.13)
  the two profiles are of different devices: /device:TPU:0 before, /device:TPU:3 now
where the time goes in v1:
time: 35.1 us; the launch traced here: 34.8 us
  Pallas kernels  31 us (88%)
  local copies, waits for them, and re-layouts  3.69 us (11%)
    pallas_call x1, Pallas kernels, local(): pl.pallas_call(functools.partial(project_kernel, cfg), out_shape=jax.Shap...  16.4 us
    pallas_call x1, Pallas kernels, local(): pl.pallas_call(functools.partial(attend_kernel, cfg), out_shape=jax.Shape...  14.6 us
    unnamed x12, local copies, waits for them, and re-layouts  2.13 us
    transpose x1, local copies, waits for them, and re-layouts, local(): q_rows = split.transpose(2, 0, 3, 1, 4).reshape(kv, rows, depth)  0.76 us
    reshape x1, local copies, waits for them, and re-layouts, local(): ctx_lens.reshape(reqs, 1)  0.73 us

profile of v1, /device:TPU:3, one launch (start us, length us, event | category | flops | bytes accessed | tf_op | source)
XLA Modules:
  0.0 34.8 jit_solution(6185193644919392474)
XLA Ops:
  0.0 0.8 %copy.20 = bf16[2,4,6,2,128]{4,3,2,1,0:T(2,128)(2,1)S(1)} copy(bf16[2,4,6,2,128]{4,3,1,2,0:T(2,128)(2,1)} %bitcast.38) | data formatting | bytes 49152 | tf_op jit(solution)/shard_map/transpose | solution.py:287
  0.8 0.7 %copy.21.len_ref = s32[8,1]{1,0:T(8,128)S(1)} copy(s32[8,1]{0,1:T(1,128)} %bitcast.42) | data formatting | bytes 64 | tf_op jit(solution)/shard_map/reshape | solution.py:310
  1.5 0.0 copy-start
  1.5 0.8 %copy-done = s32[8,1024]{1,0:T(8,128)S(1)} copy-done((s32[8,1024]{1,0:T(8,128)S(1)}, s32[8,1024]{1,0:T(8,128)}, u32[]{:S(2)}) %copy-start) | copy-done | bytes 32792
  2.2 0.0 copy-start.1
  2.3 0.8 %copy-done.1 = s32[8,1024]{1,0:T(8,128)S(1)} copy-done((s32[8,1024]{1,0:T(8,128)S(1)}, s32[8,1024]{1,0:T(8,128)}, u32[]{:S(2)}) %copy-start.1) | copy-done | bytes 32792
  3.0 0.0 copy-start.2
  3.0 0.0 copy-start.3
  3.0 0.0 copy-start.4
  3.0 14.6 %attend.1.part_ref = f32[4,48,128]{2,1,0:T(8,128)S(1)} custom-call(bf16[2,48,128]{2,1,0:T(8,128)(2,1)S(1)} %bitcast.34, s32[8,1024]{1,0:T(8,128)S(1)} %copy-done, s32[8,1024]{1,0:T(8,128)S(1)} %copy-done.1, s32[8,1]{1,0:T(8,128)S(1)} %copy.21.len_ref, bf16[2,32768,128]{2,1,0:T(8,128)(2,1)} %bitcast.35, bf16[2,32768,128]{2,1,0:T(8,128)(2,1)} %bitcast.36), custom_call_target="tpu_custom_call" | custom-call | tf_op jit(solution)/shard_map/attend/pallas_call | solution.py:289
  17.6 0.0 copy-done.2
  17.7 0.0 copy-done.3
  17.8 0.0 copy-done.4
  17.8 16.4 %project.1 = bf16[2,1536]{1,0:T(2,128)(2,1)S(1)} custom-call(f32[4,48,128]{2,1,0:T(8,128)S(1)} %attend.1.part_ref, f32[4,24,128]{2,1,0:T(8,128)S(1)} %bitcast.31, f32[4,24,128]{2,1,0:T(8,128)S(1)} %bitcast.32, f32[4,24,128]{2,1,0:T(8,128)S(1)} %bitcast.33, bf16[6144,1536]{1,0:T(8,128)(2,1)} %w_ref.1), custom_call_target="tpu_custom_call" | custom-call | tf_op jit(solution)/shard_map/project/pallas_call | solution.py:330
  34.2 0.6 %copy.30 = bf16[2,1536]{1,0:T(2,128)(2,1)} copy(bf16[2,1536]{1,0:T(2,128)(2,1)S(1)} %project.1) | data formatting | bytes 12288
  (8 shorter events, 0.1 us)
Async XLA Ops:
  1.5 0.8 %copy-start = (s32[8,1024]{1,0:T(8,128)S(1)}, s32[8,1024]{1,0:T(8,128)}, u32[]{:S(2)}) copy-start(s32[8,1024]{1,0:T(8,128)} %owner_ref.1) | copy-start | bytes 98308
  2.2 0.8 %copy-start.1 = (s32[8,1024]{1,0:T(8,128)S(1)}, s32[8,1024]{1,0:T(8,128)}, u32[]{:S(2)}) copy-start(s32[8,1024]{1,0:T(8,128)} %slot_ref.1) | copy-start | bytes 98308
  3.0 14.6 %copy-start.2 = (bf16[8,12,128]{2,0,1:T(8,128)(2,1)S(1)}, bf16[8,12,128]{2,0,1:T(8,128)(2,1)}, u32[]{:S(2)}) copy-start(bf16[8,12,128]{2,0,1:T(8,128)(2,1)} %param.9) | copy-start | bytes 73732
  3.0 14.7 %copy-start.3 = (bf16[2,8,128]{2,1,0:T(8,128)(2,1)S(1)}, bf16[2,8,128]{2,1,0:T(8,128)(2,1)}, u32[]{:S(2)}) copy-start(bf16[2,8,128]{2,1,0:T(8,128)(2,1)} %param.12) | copy-start | bytes 12292
  3.0 14.7 %copy-start.4 = (bf16[2,8,128]{2,1,0:T(8,128)(2,1)S(1)}, bf16[2,8,128]{2,1,0:T(8,128)(2,1)}, u32[]{:S(2)}) copy-start(bf16[2,8,128]{2,1,0:T(8,128)(2,1)} %param.13) | copy-start | bytes 12292

commit v2 on v1

v2 whole, which is shorter than its diff:
```python
import functools
import math

import jax
import jax.numpy as jnp
from jax import lax
from jax.experimental import pallas as pl
from jax.experimental.pallas import tpu as pltpu
from jax.sharding import PartitionSpec as P

MESH = pl.DeviceIdType.MESH
very_low = -1e30
NT = (((1,), (1,)), ((), ()))


def round_up(value, unit):
    return (value + unit - 1) // unit * unit


def whole_kernel(
    cfg, q_in, owner_in, slot_in, len_in, key_in, value_in, k_ref, v_ref, w_ref, y_ref,
    q_ref, owner_ref, slot_ref, len_ref, key_ref, value_ref, small_sem, wide_q,
    buf, s_ref, tok, mx, acc, lsum, bsem,
    wbuf, part_ref, got, mine, rows_in, lhs, total, wsem, send_a, recv_a, send_b, recv_b,
):
    pages, heads, page_rows, group, ahead, factor = cfg
    reqs, max_pages = owner_ref.shape
    buffers, kv, tokens, depth = buf.shape
    chunks = s_ref.shape[0]
    rows = group * reqs
    per_chunk = tokens // page_rows
    pieces, piece_rows = wbuf.shape[0], wbuf.shape[1]
    own_reqs = reqs // pages
    out_reqs = reqs // heads
    shares = pages // heads
    half = part_ref.shape[1] // 2
    head_count = kv * group
    replica = lax.axis_index("group")
    p = lax.axis_index("pages")
    h = lax.axis_index("heads")

    def stream(source, c, i):
        at = lax.rem(i, buffers)
        start = pl.multiple_of(c * tokens, tokens)
        return pltpu.make_async_copy(source.at[:, pl.ds(start, tokens)], buf.at[at], bsem.at[at])

    def weight_copy(i):
        return pltpu.make_async_copy(
            w_ref.at[pl.ds(pl.multiple_of(i * piece_rows, piece_rows), piece_rows)], wbuf.at[i], wsem.at[i]
        )

    small = [
        pltpu.make_async_copy(source, target, small_sem.at[i])
        for i, (source, target) in enumerate(
            (
                (owner_in, owner_ref),
                (slot_in, slot_ref),
                (len_in, len_ref),
                (q_in, q_ref),
                (key_in, key_ref),
                (value_in, value_ref),
            )
        )
    ]
    for copy in small:
        copy.start()
    for i in range(ahead):
        stream(k_ref, i, i).start()

    barrier = pltpu.get_barrier_semaphore()
    count = pages * heads
    for k in range(1, count):
        other = lax.rem(p * heads + h + k, count)
        pl.semaphore_signal(
            barrier, inc=1, device_id=(replica, other // heads, lax.rem(other, heads)), device_id_type=MESH
        )
    for copy in small:
        copy.wait()

    wide_q[...] = jnp.zeros_like(wide_q)
    for n in range(kv):
        wide_q[n * rows : (n + 1) * rows, n * depth : (n + 1) * depth] = q_ref[n]
    page_start = lax.broadcasted_iota(jnp.int32, (1, max_pages), 1) * page_rows
    slot = slot_ref[...]
    upper = jnp.where(owner_ref[...] == p, slot // per_chunk, -1)
    lower = slot % per_chunk
    upper_id = lax.broadcasted_iota(jnp.int32, (chunks, max_pages), 0)
    lower_id = lax.broadcasted_iota(jnp.int32, (per_chunk, max_pages), 0)
    table = jnp.zeros((2 * chunks, per_chunk), jnp.float32)
    for r in range(reqs):
        hit = upper[r : r + 1] == upper_id
        live = jnp.clip(len_ref[r] - page_start, 0, page_rows).astype(jnp.float32)
        left = jnp.concatenate(
            [jnp.where(hit, float(r + 1), 0.0), jnp.where(hit, live, 0.0)], axis=0
        ).astype(jnp.bfloat16)
        right = jnp.where(lower[r : r + 1] == lower_id, 1.0, 0.0).astype(jnp.bfloat16)
        table += lax.dot_general(left, right, NT, preferred_element_type=jnp.float32)
    spread = jnp.where(
        lax.broadcasted_iota(jnp.int32, (per_chunk, tokens), 1) // page_rows
        == lax.broadcasted_iota(jnp.int32, (per_chunk, tokens), 0),
        1.0,
        0.0,
    ).astype(jnp.bfloat16)
    wide = jnp.dot(table.astype(jnp.bfloat16), spread, preferred_element_type=jnp.float32)
    row_number = (lax.broadcasted_iota(jnp.int32, (chunks, tokens), 1) % page_rows).astype(jnp.float32)
    token_owner = jnp.where(row_number < wide[chunks:], wide[:chunks], 0.0)
    for c in range(chunks):
        tok[c] = jnp.broadcast_to(token_owner[c : c + 1], (8, tokens))

    req_id = (lax.broadcasted_iota(jnp.int32, (reqs, 128), 0) + 1).astype(jnp.float32)
    req_groups = reqs // 8
    mx[...] = jnp.full_like(mx, very_low)
    sub = min(tokens, 512)

    def score_chunk(c, carry):
        pl.when(c + ahead < chunks)(lambda: stream(k_ref, c + ahead, c + ahead).start())
        pl.when(c + ahead >= chunks)(lambda: stream(v_ref, c + ahead - chunks, c + ahead).start())
        at_buf = lax.rem(c, buffers)
        stream(k_ref, c, c).wait()
        groups = kv * rows // 8
        best = [mx[g * 8 // rows, g * 8 % rows : g * 8 % rows + 8] for g in range(groups)]
        for b in range(tokens // sub):
            keys = jnp.concatenate([buf[at_buf, n, b * sub : (b + 1) * sub, :] for n in range(kv)], axis=1)
            s = lax.dot_general(wide_q[...], keys, NT, preferred_element_type=jnp.float32)
            for t in range(sub // 128):
                at = b * sub + t * 128
                who = tok[c, :, at : at + 128]
                hits = [who == req_id[8 * j : 8 * j + 8] for j in range(req_groups)]
                for g in range(groups):
                    kept = jnp.where(
                        hits[g % req_groups], s[8 * g : 8 * g + 8, t * 128 : t * 128 + 128], very_low
                    )
                    s_ref[c, g * 8 // rows, g * 8 % rows : g * 8 % rows + 8, at : at + 128] = kept
                    best[g] = jnp.maximum(best[g], kept)
        for g in range(groups):
            mx[g * 8 // rows, g * 8 % rows : g * 8 % rows + 8] = best[g]
        return carry

    lax.fori_loop(0, chunks, score_chunk, 0)

    row_id = lax.broadcasted_iota(jnp.int32, (rows, 128), 0)
    lane = lax.broadcasted_iota(jnp.int32, (rows, 128), 1)
    mine_row = lax.rem(row_id, reqs) // own_reqs == p
    for n in range(kv):
        keys = jnp.concatenate([key_ref[n].astype(jnp.float32)] * group, axis=0)
        values = jnp.concatenate([value_ref[n].astype(jnp.float32)] * group, axis=0)
        self_score = jnp.sum(q_ref[n].astype(jnp.float32) * keys, axis=1, keepdims=True)
        top = jnp.max(mx[n], axis=1, keepdims=True)
        top = jnp.where(mine_row, jnp.maximum(top, self_score), top)
        take = jnp.where(mine_row, jnp.exp2((self_score - top) * factor), 0.0)
        mx[n] = top
        acc[n] = take * values
        lsum[n] = jnp.where(lane == 0, take, 0.0)

    def value_chunk(c, carry):
        i = chunks + c
        pl.when(c + ahead < chunks)(lambda: stream(v_ref, c + ahead, i + ahead).start())
        pl.when(jnp.logical_and(c + ahead >= chunks, c + ahead < chunks + pieces))(
            lambda: weight_copy(c + ahead - chunks).start()
        )
        at_buf = lax.rem(i, buffers)
        stream(v_ref, c, i).wait()
        peaks = [mx[n] for n in range(kv)]
        sums = [lsum[n] for n in range(kv)]
        outs = [acc[n] for n in range(kv)]
        for b in range(tokens // sub):
            stack = []
            for n in range(kv):
                parts = []
                for t in range(sub // 128):
                    at = b * sub + t * 128
                    w = jnp.exp2((s_ref[c, n, :, at : at + 128] - peaks[n]) * factor)
                    sums[n] += w
                    parts.append(w.astype(jnp.bfloat16))
                stack.append(jnp.concatenate(parts, axis=1))
            values = jnp.concatenate([buf[at_buf, n, b * sub : (b + 1) * sub, :] for n in range(kv)], axis=1)
            both = jnp.dot(jnp.concatenate(stack, axis=0), values, preferred_element_type=jnp.float32)
            for n in range(kv):
                outs[n] += both[n * rows : (n + 1) * rows, n * depth : (n + 1) * depth]
        for n in range(kv):
            lsum[n] = sums[n]
            acc[n] = outs[n]
        return carry

    lax.fori_loop(0, chunks, value_chunk, 0)
    for i in range(min(ahead, pieces), pieces):
        weight_copy(i).start()

    part_ref[...] = jnp.zeros_like(part_ref)
    for n in range(kv):
        stats = jnp.where(lane == 0, mx[n], jnp.sum(lsum[n], axis=1, keepdims=True))
        out = acc[n]
        for b in range(pages):
            for g in range(group):
                here = slice(g * reqs + b * own_reqs, g * reqs + (b + 1) * own_reqs)
                first = (n * group + g) * own_reqs
                part_ref[b, first : first + own_reqs, :] = out[here]
                part_ref[b, half + first : half + first + own_reqs, :] = stats[here]
    pl.semaphore_wait(barrier, count - 1)

    def exchange(k):
        to = lax.rem(p + k, pages)
        return pltpu.make_async_remote_copy(
            src_ref=part_ref.at[to],
            dst_ref=got.at[k - 1],
            send_sem=send_a.at[k - 1],
            recv_sem=recv_a.at[k - 1],
            device_id=(replica, to, h),
            device_id_type=MESH,
        )

    for k in range(1, pages):
        exchange(k).start()
    for k in range(1, pages):
        exchange(k).wait_recv()

    tops = [part_ref[p, half:, 0:1]] + [got[k, half:, 0:1] for k in range(pages - 1)]
    sums = [part_ref[p, half:, 1:2]] + [got[k, half:, 1:2] for k in range(pages - 1)]
    outs = [part_ref[p, :half]] + [got[k, :half] for k in range(pages - 1)]
    peak = tops[0]
    for t in tops[1:]:
        peak = jnp.maximum(peak, t)
    out = jnp.zeros_like(outs[0])
    weight = jnp.zeros_like(peak)
    for t, s, o in zip(tops, sums, outs):
        f = jnp.exp2((t - peak) * factor)
        out += f * o
        weight += f * s
    attended = (out / jnp.where(weight > 0.0, weight, 1.0)).astype(jnp.bfloat16)
    mine[...] = jnp.zeros_like(mine)
    mine[0:half, :] = attended

    target = p // shares
    place = lax.rem(p, shares) * heads + h

    def hand_over(k):
        to = lax.rem(p + k, pages)
        return pltpu.make_async_remote_copy(
            src_ref=mine,
            dst_ref=rows_in.at[place],
            send_sem=send_b.at[k],
            recv_sem=recv_b.at[place],
            device_id=(replica, to, target),
            device_id_type=MESH,
        )

    for k in range(pages):
        if k == 0:
            pl.when(target != h)(lambda: hand_over(0).start())

            @pl.when(target == h)
            def _():
                rows_in[place] = mine[...]
        else:
            hand_over(k).start()

    def arrival(source):
        return pltpu.make_async_remote_copy(
            src_ref=mine,
            dst_ref=rows_in.at[source],
            send_sem=send_b.at[0],
            recv_sem=recv_b.at[source],
            device_id=(replica, p, target),
            device_id_type=MESH,
        )

    for source in range(shares * heads):
        remote = jnp.logical_or(target != h, place != source)
        pl.when(remote)(lambda source=source: arrival(source).wait_recv())

    lhs[...] = jnp.zeros_like(lhs)
    per_piece = piece_rows // depth
    for source in range(shares * heads):
        first = source // heads * own_reqs
        block = rows_in[source].astype(jnp.float32)
        for n in range(head_count):
            which = source % heads * head_count + n
            col = which % per_piece * depth
            lhs[which // per_piece, first : first + own_reqs, col : col + depth] = block[
                n * own_reqs : (n + 1) * own_reqs
            ]
    total[...] = jnp.zeros_like(total)

    def multiply(i, carry):
        weight_copy(i).wait()
        total[...] += jnp.dot(
            lhs[i].astype(jnp.bfloat16), wbuf[i], preferred_element_type=jnp.float32
        )
        return carry

    lax.fori_loop(0, pieces, multiply, 0)
    y_ref[...] = total[0:out_reqs].astype(jnp.bfloat16)
    for k in range(1, pages):
        exchange(k).wait_send()
    pl.when(target != h)(lambda: hand_over(0).wait_send())
    for k in range(1, pages):
        hand_over(k).wait_send()


def local(sizes, queries, k_cache, v_cache, new_key, new_value, ctx_lens, page_owner, page_slot, out_weight):
    pages, heads = sizes
    kv, slots, page_rows, depth = k_cache.shape
    reqs, q_local, _ = queries.shape
    group = q_local // kv
    factor = math.log2(math.e) / math.sqrt(depth)
    per_chunk = math.gcd(slots, 128)
    chunks = slots // per_chunk
    tokens = per_chunk * page_rows
    rows = group * reqs
    half = round_up(kv * group * (reqs // pages), 8)
    model, columns = out_weight.shape
    pieces = math.gcd(model // depth, 8)
    sources = pages // heads * heads
    lines = round_up(half, 16)
    ahead = min(6, chunks)
    vmem = pl.BlockSpec(memory_space=pltpu.VMEM)
    hbm = pl.BlockSpec(memory_space=pl.ANY)
    return pl.pallas_call(
        functools.partial(whole_kernel, (pages, heads, page_rows, group, ahead, factor)),
        out_shape=jax.ShapeDtypeStruct((reqs // heads, columns), jnp.bfloat16),
        in_specs=[hbm] * 9,
        out_specs=vmem,
        scratch_shapes=[
            pltpu.VMEM((kv, rows, depth), jnp.bfloat16),
            pltpu.VMEM(page_owner.shape, jnp.int32),
            pltpu.VMEM(page_slot.shape, jnp.int32),
            pltpu.SMEM(ctx_lens.shape, jnp.int32),
            pltpu.VMEM(new_key.shape, jnp.bfloat16),
            pltpu.VMEM(new_value.shape, jnp.bfloat16),
            pltpu.SemaphoreType.DMA((6,)),
            pltpu.VMEM((kv * rows, kv * depth), jnp.bfloat16),
            pltpu.VMEM((ahead + 2, kv, tokens, depth), jnp.bfloat16),
            pltpu.VMEM((chunks, kv, rows, tokens), jnp.float32),
            pltpu.VMEM((chunks, 8, tokens), jnp.float32),
            pltpu.VMEM((kv, rows, 128), jnp.float32),
            pltpu.VMEM((kv, rows, depth), jnp.float32),
            pltpu.VMEM((kv, rows, 128), jnp.float32),
            pltpu.SemaphoreType.DMA((ahead + 2,)),
            pltpu.VMEM((pieces, model // pieces, columns), jnp.bfloat16),
            pltpu.VMEM((pages, 2 * half, depth), jnp.float32),
            pltpu.VMEM((pages - 1, 2 * half, depth), jnp.float32),
            pltpu.VMEM((lines, depth), jnp.bfloat16),
            pltpu.VMEM((sources, lines, depth), jnp.bfloat16),
            pltpu.VMEM((pieces, 8, model // pieces), jnp.float32),
            pltpu.VMEM((8, columns), jnp.float32),
            pltpu.SemaphoreType.DMA((pieces,)),
            pltpu.SemaphoreType.DMA((pages - 1,)),
            pltpu.SemaphoreType.DMA((pages - 1,)),
            pltpu.SemaphoreType.DMA((pages,)),
            pltpu.SemaphoreType.DMA((sources,)),
        ],
        compiler_params=pltpu.CompilerParams(
            collective_id=0, has_side_effects=True, vmem_limit_bytes=56 * 1024 * 1024
        ),
        name="decode",
    )(
        queries.transpose(1, 0, 2).reshape(kv, rows, depth),
        page_owner,
        page_slot,
        ctx_lens,
        new_key,
        new_value,
        k_cache.reshape(kv, slots * page_rows, depth),
        v_cache.reshape(kv, slots * page_rows, depth),
        out_weight,
    )


def solution(mesh):
    placed = (
        P("group", "heads", None),
        P("heads", ("group", "pages"), None, None),
        P("heads", ("group", "pages"), None, None),
        P("heads", "group", None),
        P("heads", "group", None),
        P("group"),
        P("group", None),
        P("group", None),
        P(None, "pages"),
    )
    sizes = (mesh.shape["pages"], mesh.shape["heads"])
    return jax.shard_map(
        functools.partial(local, sizes),
        mesh=mesh,
        in_specs=placed,
        out_specs=P(("group", "heads"), "pages"),
        check_vma=False,
    )
```

time: 35.1 us -> 32.4 us (0.923)
  the two profiles are of different devices: /device:TPU:3 before, /device:TPU:0 now
where the time goes in v2:
time: 32.4 us; the launch traced here: 32.2 us
  Pallas kernels  30.9 us (95%)
  local copies, waits for them, and re-layouts  1.29 us (4%)
    pallas_call x1, Pallas kernels, local(): pl.pallas_call(functools.partial(whole_kernel, (pages, heads, page_rows,...  30.9 us
    unnamed x1, local copies, waits for them, and re-layouts  1.29 us

profile of v2, /device:TPU:0, one launch (start us, length us, event | category | flops | bytes accessed | tf_op | source)
XLA Modules:
  0.0 32.2 jit_solution(16390202426138413958)
XLA Ops:
  0.0 30.9 %decode.1 = bf16[2,1536]{1,0:T(2,128)(2,1)} custom-call(bf16[2,48,128]{2,1,0:T(8,128)(2,1)} %bitcast.7, s32[8,1024]{1,0:T(8,128)} %owner_in.1, s32[8,1024]{1,0:T(8,128)} %slot_in.1, s32[8]{0:T(128)} %len_in.1, bf16[2,8,128]{2,1,0:T(8,128)(2,1)} %key_in.1, bf16[2,8,128]{2,1,0:T(8,128)(2,1)} %value_in.1, bf16[2,32768,128]{2,1,0:T(8,128)(2,1)} %bitcast.5, ...), custom_call_target="tpu_custom_call" | custom-call | tf_op jit(solution)/shard_map/decode/pallas_call | solution.py:318
  30.9 1.3 %copy.11 = bf16[2,1536]{1,0:T(2,128)(2,1)} copy(bf16[2,1536]{1,0:T(2,128)(2,1)} %decode.1) | data formatting | bytes 12288
